TPU v7x, 512 devices: a whole 4x8x8 slice. The times are simulated.
512 devices in a mesh: vocab: 64 (over z, y), pipe: 8 (over x, core).
Axes of the slice: x: 4, y: 8, z: 8, core: 2. Of those that a mesh axis runs over, the one named last changes fastest.
Arguments:
- hidden_a: bfloat16 [2048, 4096], P('pipe', 'vocab'), parts along dimension 0, may hold values from -8 to 8, as said below
- labels_a: int32 [2048], P('pipe'), parts along dimension 0, may hold values from 0 to 32767
- hidden_b: bfloat16 [2048, 4096], P('pipe', 'vocab'), parts along dimension 0, may hold values from -8 to 8, as said below
- labels_b: int32 [2048], P('pipe'), parts along dimension 0, may hold values from 0 to 32767
- loss_cotangent: float32 [2048], P('pipe'), parts along dimension 0, may hold values from -192 to 192
- out_weight: bfloat16 [32768, 32768], P('pipe', 'vocab'), parts along dimension 0, may hold values from -0.28125 to 0.28125, as said below
Outputs:
- logits_a: bfloat16 [2048, 32768], P('pipe', 'vocab'), parts along dimension 0
- loss_a: float32 [2048], P('pipe'), parts along dimension 0
- amax_scale: float32 [8], P('pipe'), parts along dimension 0
- grad_hidden_b: bfloat16 [2048, 4096], P('pipe', 'vocab'), parts along dimension 0
There are 8 independent parts, one for each index of `pipe`. A program takes and returns all parts, laid end to end along the dimension named above; each array names one. Nothing has to cross between parts.
Inputs may be any that keep to these rules, and one draw needn't show every extreme that they name: `hidden_a`: hidden states of order one. `hidden_b`: hidden states of order one. `out_weight`: entries of scale 3 over the square root of 4096.
All inputs are finite; a program needn't handle non-finite values. Where the computation divides by a largest or mean magnitude, that divisor is 1e-20 or more.
Results may differ from a plain program's by a relative error of at most 0.0048.
Values may be sent and summed in bfloat16 or wider, within the bound.
No kernel may reach another device: no remote copies, remote signals or barrier semaphores. Data moves between devices by JAX's collectives and lax.ppermute only.
A program may use at most 64 MiB of HBM per device.

v0:
```python
import jax
import jax.numpy as jnp
from jax import lax
from jax.sharding import Mesh
from jax.sharding import PartitionSpec as P

VOCAB = ("vocab_0", "vocab_1")


def turned_gather(arrays, axis, dims):
    turned = [jnp.moveaxis(a, dim, 0) for a, dim in zip(arrays, dims)]
    both = jnp.concatenate([t.reshape(len(t), -1) for t in turned], axis=1)
    filled, at, gathered = (lax.all_gather(both, axis, axis=0, tiled=True), 0, [])
    for t, dim in zip(turned, dims):
        slab = filled[:, at : at + t[0].size].reshape(-1, *t.shape[1:])
        gathered.append(jnp.moveaxis(slab, 0, dim))
        at += t[0].size
    return tuple(gathered)


def collected_together(x, axis):
    leaves = jax.tree.leaves(x)
    order = sorted(range(len(leaves)), key=lambda k: -leaves[k].size)
    width = (1, *leaves[order[0]].shape)[-1]
    lines = [
        jnp.pad(leaves[k].reshape(-1), (0, -leaves[k].size % width)).reshape(-1, width)
        for k in order
    ]
    both, at, found = (lax.all_gather(jnp.concatenate(lines), axis), 0, {})
    for k, line in zip(order, lines):
        slab = both[:, at : at + len(line)].reshape(len(both), -1)
        found[k] = slab[:, : leaves[k].size].reshape(-1, *leaves[k].shape)
        at += len(line)
    numbers = iter(range(len(leaves)))
    return jax.tree.map(lambda _: found[next(numbers)], x)


def joined_all(x, axes, combine):
    for axis in axes:
        pieces = collected_together(x, axis)
        x = jax.tree.map(lambda part: part[0], pieces)
        for k in range(1, lax.axis_size(axis)):
            x = combine(x, jax.tree.map(lambda part: part[k], pieces))
    return x


def from_everyone(x, axis):
    devices = lax.axis_size(axis)
    return lax.all_to_all(jnp.broadcast_to(x[None], (devices, *x.shape)), axis, 0, 0, tiled=True)


def all_in_one(x, axis):
    leaves = jax.tree.leaves(x)
    order = sorted(range(len(leaves)), key=lambda k: -leaves[k].size)
    width = (1, *leaves[order[0]].shape)[-1]
    lines = [
        jnp.pad(leaves[k].reshape(-1), (0, -leaves[k].size % width)).reshape(-1, width)
        for k in order
    ]
    both, at, found = (from_everyone(jnp.concatenate(lines), axis), 0, {})
    for k, line in zip(order, lines):
        slab = both[:, at : at + len(line)].reshape(len(both), -1)
        found[k] = slab[:, : leaves[k].size].reshape(-1, *leaves[k].shape)
        at += len(line)
    numbers = iter(range(len(leaves)))
    return jax.tree.map(lambda _: found[next(numbers)], x)


def joined_by_halves(pieces, combine):
    while len(jax.tree.leaves(pieces)[0]) > 1:
        pieces = jax.vmap(combine)(
            *(jax.tree.map(lambda part: part[side::2], pieces) for side in (0, 1))
        )
    return jax.tree.map(lambda part: part[0], pieces)


def merged(x, axis, combine):
    pieces = all_in_one(x, axis)
    return joined_by_halves(pieces, combine)


def scatter_axes(x, axes, dim):
    for axis in axes:
        x = lax.psum_scatter(x, axis, scatter_dimension=dim, tiled=True)
    return x


def combine_forward(earlier, later):
    highest = jnp.maximum(earlier[0], later[0])
    summed = earlier[1] * jnp.exp(earlier[0] - highest) + later[1] * jnp.exp(later[0] - highest)
    return (highest, summed, earlier[2] + later[2], jnp.maximum(earlier[3], later[3]))


def combine_backward(earlier, later):
    highest = jnp.maximum(earlier[0], later[0])
    summed = earlier[1] * jnp.exp(earlier[0] - highest) + later[1] * jnp.exp(later[0] - highest)
    return (highest, summed)


def shards(hidden_a, labels_a, hidden_b, labels_b, loss_cotangent, out_weight):
    vocab_rows = out_weight.shape[1]
    offset = lax.axis_index(VOCAB) * vocab_rows
    portions = turned_gather((hidden_a, hidden_b), VOCAB, (1, 1))
    scores_a = jnp.dot(portions[0], out_weight, preferred_element_type=jnp.float32)
    scores_b = jnp.dot(portions[1], out_weight, preferred_element_type=jnp.float32)
    columns_a = offset + lax.broadcasted_iota(jnp.int32, scores_a.shape, 1)
    columns_b = offset + lax.broadcasted_iota(jnp.int32, scores_b.shape, 1)
    label_local = jnp.sum(jnp.where(columns_a == labels_a[:, None], scores_a, 0.0), axis=1)
    row_peak_a = jnp.max(scores_a, axis=1)
    abs_peak = jnp.max(jnp.abs(scores_a)).reshape(1)
    row_peak_b = jnp.max(scores_b, axis=1)
    own_total_a = jnp.sum(jnp.exp(scores_a - row_peak_a[:, None]), axis=1)
    peak_a, total_a, label_a, largest = joined_all(
        (row_peak_a, own_total_a, label_local, abs_peak), VOCAB, combine_forward
    )
    own_total_b = jnp.sum(jnp.exp(scores_b - row_peak_b[:, None]), axis=1)
    peak_b, total_b = merged((row_peak_b, own_total_b), VOCAB, combine_backward)
    loss_a = jnp.log(total_a) + peak_a - label_a
    amax_scale = (448.0 / largest).astype(jnp.float32)
    onehot = (columns_b == labels_b[:, None]).astype(jnp.float32)
    probs = jnp.exp(scores_b - peak_b[:, None]) / total_b[:, None]
    dlogits_b = ((probs - onehot) * loss_cotangent[:, None]).astype(jnp.bfloat16)
    grad_terms = lax.dot_general(
        dlogits_b, out_weight, (((1,), (1,)), ((), ())), preferred_element_type=jnp.float32
    )
    grad_hidden_b = scatter_axes(grad_terms, VOCAB, 1).astype(jnp.bfloat16)
    return (scores_a.astype(jnp.bfloat16), loss_a, amax_scale, grad_hidden_b)


def solution(mesh):
    finer = Mesh(mesh.devices.reshape(8, 8, mesh.shape["pipe"]), ("vocab_0", "vocab_1", "pipe"))
    placed = (P("pipe", VOCAB), P("pipe"), P("pipe", VOCAB), P("pipe"), P("pipe"), P("pipe", VOCAB))
    return jax.shard_map(
        shards,
        mesh=finer,
        in_specs=placed,
        out_specs=(P("pipe", VOCAB), P("pipe"), P("pipe"), P("pipe", VOCAB)),
        check_vma=False,
    )
```

profile of v0, /device:TPU:2, one launch (start us, length us, event | category | flops | bytes accessed | tf_op | source)
XLA Modules:
  0.0 236.3 jit_solution(9642558782417592460)
XLA Ops:
  7.2 0.0 all-gather.6.cloned.1.call-start
  7.2 1.4 pad_maximum_fusion
  8.6 0.0 all-gather.6.cloned.1.call-update
  8.6 0.0 copy-start
  8.7 0.0 copy-start.1
  8.7 94.4 %all-gather.6.cloned.1.call-done = bf16[4096,512]{1,0:T(8,128)(2,1)} async-done(((bf16[64,512]{1,0:T(8,128)(2,1)}), bf16[4096,512]{1,0:T(8,128)(2,1)}) %all-gather.6.cloned.1.call-update) | async-done | bytes 4194320 | tf_op jit(solution)/shard_map/all_gather | solution.py:13
  103.1 4.2 %fusion.61 = (f32[256]{0:T(256)S(1)}, f32[256,512]{1,0:T(8,128)S(1)}) fusion(bf16[4096,512]{1,0:T(8,128)(2,1)} %param.11, bf16[4096,512]{1,0:T(8,128)(2,1)} %all-gather.6.cloned.1.call-done), kind=kOutput, calls=%fused_computation.120 | convolution fusion | flops 1073872640 | bytes 6816768 | tf_op jit(solution)/shard_map/dot_general | solution.py:105
  107.2 0.2 exponential_reduce_fusion
  107.5 0.7 broadcast_in_dim.7
  108.2 8.3 %all-to-all-start = ((f32[64,2,256]{2,1,0:T(2,128)}), f32[64,2,256]{2,1,0:T(2,128)S(1)}, u32[]{:S(2)}, u32[]{:S(2)}) async-start(f32[64,2,256]{2,1,0:T(2,128)} %broadcast_in_dim.7), calls=%async_computation | async-start | bytes 262144 | tf_op jit(solution)/shard_map/all_to_all | solution.py:49
  116.5 0.0 reduce-scatter.5.cloned.1.call-start
  116.6 12.6 %all-to-all-done = f32[64,2,256]{2,1,0:T(2,128)S(1)} async-done(((f32[64,2,256]{2,1,0:T(2,128)}), f32[64,2,256]{2,1,0:T(2,128)S(1)}, u32[]{:S(2)}, u32[]{:S(2)}) %all-to-all-start) | async-done | bytes 131104 | tf_op jit(solution)/shard_map/all_to_all | solution.py:49
  129.2 0.1 fusion.55
  129.9 5.5 %fusion.4 = f32[256,4096]{1,0:T(8,128)} fusion(bf16[4096,512]{1,0:T(8,128)(2,1)} %param.11, f32[256,512]{1,0:T(8,128)S(1)} %get-tuple-element.68, f32[256]{0:T(256)S(1)} %copy-done, f32[256]{0:T(256)S(1)} %bitcast.212, f32[256]{0:T(256)S(1)} %bitcast.213, s32[512]{0:T(512)S(1)} %iota_add_fusion, s32[256]{0:T(256)S(1)} %copy-done.1), kind=kOutput, calls=%fused_computation.9 | convolution fusion | flops 1074659328 | bytes 8919040 | tf_op jit(solution)/shard_map/dot_general | solution.py:123
  135.4 0.0 reduce-scatter.5.cloned.1.call-update
  135.4 0.0 copy-start.2
  135.4 0.0 reduce-scatter.7.cloned.1.call-start
  135.5 4.2 %fusion.60 = (f32[256]{0:T(256)S(1)}, f32[256,512]{1,0:T(8,128)S(1)}) fusion(bf16[4096,512]{1,0:T(8,128)(2,1)} %param.11, bf16[4096,512]{1,0:T(8,128)(2,1)} %all-gather.6.cloned.1.call-done), kind=kOutput, calls=%fused_computation.119 | convolution fusion | flops 1073872640 | bytes 6816768 | tf_op jit(solution)/shard_map/dot_general | solution.py:104
  139.6 0.0 copy-done.2
  139.7 1.5 exponential_reduce_fusion.1
  141.2 0.7 pad.7
  141.9 25.2 %all-gather.2 = f32[8,4,256]{2,1,0:T(4,128)S(1)} all-gather(f32[1,4,256]{2,1,0:T(4,128)S(1)} %maximum_bitcast_fusion), channel_id=2, replica_groups=mesh['vocab_0'=8,'vocab_1'=8,'pipe'=8] {'vocab_0'}, dimensions={0}, use_global_device_ids=true | all-gather | bytes 36864 | tf_op jit(solution)/shard_map/all_gather | solution.py:29
  167.1 0.6 fusion.59
  172.8 13.3 %reduce-scatter.5.cloned.1.call-done = f32[256,512]{1,0:T(8,128)} async-done(((f32[256,4096]{1,0:T(8,128)}), f32[256,512]{1,0:T(8,128)}) %reduce-scatter.5.cloned.1.call-update) | async-done | bytes 524304 | tf_op jit(solution)/shard_map/reduce_scatter | solution.py:84
  186.1 2.0 copy.14
  188.1 0.0 reduce-scatter.7.cloned.1.call-update
  188.2 25.7 %all-gather.3 = f32[8,4,256]{2,1,0:T(4,128)S(1)} all-gather(f32[1,4,256]{2,1,0:T(4,128)S(1)} %maximum_bitcast_fusion.1), channel_id=3, replica_groups=mesh['vocab_0'=8,'vocab_1'=8,'pipe'=8] {'vocab_1'}, dimensions={0}, use_global_device_ids=true | all-gather | bytes 36864 | tf_op jit(solution)/shard_map/all_gather | solution.py:29
  213.9 0.6 fusion.58
  219.6 0.6 add_subtract_fusion
  220.2 6.8 %reduce-scatter.7.cloned.1.call-done = f32[64,256]{1,0:T(8,128)} async-done(((f32[512,256]{1,0:T(8,128)}), f32[64,256]{1,0:T(8,128)}) %reduce-scatter.7.cloned.1.call-update) | async-done | bytes 65552
  227.0 0.9 copy.15
  228.0 0.7 copy.13
  (42 shorter events, 0.6 us)
Async XLA Ops:
  7.2 95.9 %all-gather.6.cloned.1.call-start = ((), (), s32[]{:S(2)}) async-start(), calls=%async_computation.3 | async-start | bytes 4259840 | tf_op jit(solution)/shard_map/all_gather | solution.py:13
  8.6 121.2 %copy-start = (f32[256]{0:T(256)S(1)}, f32[256]{0:T(256)}, u32[]{:S(2)}) copy-start(f32[256]{0:T(256)} %param.10) | copy-start | bytes 3076
  8.7 121.2 %copy-start.1 = (s32[256]{0:T(256)S(1)}, s32[256]{0:T(256)}, u32[]{:S(2)}) copy-start(s32[256]{0:T(256)} %param.9) | copy-start | bytes 3076
  108.2 21.0 %all-to-all-start = ((f32[64,2,256]{2,1,0:T(2,128)}), f32[64,2,256]{2,1,0:T(2,128)S(1)}, u32[]{:S(2)}, u32[]{:S(2)}) async-start(f32[64,2,256]{2,1,0:T(2,128)} %broadcast_in_dim.7), calls=%async_computation | async-start | bytes 262144 | tf_op jit(solution)/shard_map/all_to_all | solution.py:49
  116.5 69.6 %reduce-scatter.5.cloned.1.call-start = ((), (), s32[]{:S(2)}) async-start(), calls=%async_computation.4 | async-start | bytes 4718592 | tf_op jit(solution)/shard_map/reduce_scatter | solution.py:84
  135.4 4.2 %copy-start.2 = (s32[256]{0:T(256)S(1)}, s32[256]{0:T(256)}, u32[]{:S(2)}) copy-start(s32[256]{0:T(256)} %param.7) | copy-start | bytes 3076
  135.4 91.6 %reduce-scatter.7.cloned.1.call-start = ((), (), s32[]{:S(2)}) async-start(), calls=%async_computation.5 | async-start | bytes 589824
Sparse Core Ops, SparseCore 0:
  11.6 91.4 all-gather.5
  135.5 50.5 reduce-scatter.4
  188.9 38.0 reduce-scatter.6
where the time goes:
time: 237 us; the launch traced here: 236 us
  waiting for transfers between devices  127 us (54%)
  blocking collectives  50.9 us (21%)
  between operations  25.2 us (11%)
  matrix products  13.8 us (6%)
  starting transfers between devices  8.44 us (4%)
  local copies, waits for them, and re-layouts  6.81 us (3%)
  other arithmetic  3.99 us (2%)
    all_gather x1, waiting for transfers between devices, turned_gather(): lax.all_gather(both, axis, axis=0, tiled=True)  94.4 us
    all_gather x2, blocking collectives, collected_together(): both, at, found = (lax.all_gather(jnp.concatenate(lines), axis), 0, {})  50.9 us
    reduce_scatter x1, waiting for transfers between devices, scatter_axes(): x = lax.psum_scatter(x, axis, scatter_dimension=dim, tiled=True)  13.3 us
    all_to_all x1, waiting for transfers between devices, from_everyone(): lax.all_to_all(jnp.broadcast_to(x[None], (devices, *x.shape)), axis, 0, 0...  12.6 us
    all_to_all x1, starting transfers between devices, from_everyone(): lax.all_to_all(jnp.broadcast_to(x[None], (devices, *x.shape)), axis, 0, 0...  8.32 us
    unnamed x4, waiting for transfers between devices  6.9 us
    dot_general x1, matrix products, shards(): lax.dot_general(dlogits_b, out_weight, (((1,), (1,)), ((), ())), preferre...  5.51 us
  transfers between devices with their start and end apart: 4, of which 4 were waited for; matrix products, arithmetic and copies ran while one was open for 4% of the time, Pallas kernels for 0%

commit v1 on v0

--- a/solution.py
+++ b/solution.py
@@ -10,7 +10,13 @@
 def turned_gather(arrays, axis, dims):
     turned = [jnp.moveaxis(a, dim, 0) for a, dim in zip(arrays, dims)]
     both = jnp.concatenate([t.reshape(len(t), -1) for t in turned], axis=1)
-    filled, at, gathered = (lax.all_gather(both, axis, axis=0, tiled=True), 0, [])
+    filled, at, gathered = (
+        jnp.concatenate(
+            lax.all_to_all(jnp.stack([both] * lax.axis_size(axis)), axis, 0, 0), axis=0
+        ),
+        0,
+        [],
+    )
     for t, dim in zip(turned, dims):
         slab = filled[:, at : at + t[0].size].reshape(-1, *t.shape[1:])
         gathered.append(jnp.moveaxis(slab, 0, dim))

time: 237 us -> 259 us (1.093)
  the two profiles are of different devices: /device:TPU:2 before, /device:TPU:4 now
where the time goes in v1:
time: 259 us
  blocking collectives  165 us (64%)
  waiting for transfers between devices  32.9 us (13%)
  between operations  25.5 us (10%)
  starting transfers between devices  12.7 us (5%)
  matrix products  11 us (4%)
  local copies, waits for them, and re-layouts  7.87 us (3%)
  other arithmetic  3.36 us (1%)
    all_to_all x1, blocking collectives, turned_gather(): lax.all_to_all(jnp.stack([both] * lax.axis_size(axis)), axis, 0, 0)  114 us
    all_gather x2, blocking collectives, collected_together(): both, at, found = (lax.all_gather(jnp.concatenate(lines), axis), 0, {})  50.9 us
    reduce_scatter x1, waiting for transfers between devices, scatter_axes(): x = lax.psum_scatter(x, axis, scatter_dimension=dim, tiled=True)  13.4 us
    all_to_all x1, waiting for transfers between devices, from_everyone(): lax.all_to_all(jnp.broadcast_to(x[None], (devices, *x.shape)), axis, 0, 0...  12.7 us
    all_to_all x1, starting transfers between devices, from_everyone(): lax.all_to_all(jnp.broadcast_to(x[None], (devices, *x.shape)), axis, 0, 0...  12.6 us
    unnamed x3, waiting for transfers between devices  6.83 us
    dot_general x1, matrix products, shards(): lax.dot_general(dlogits_b, out_weight, (((1,), (1,)), ((), ())), preferre...  5.49 us
  transfers between devices with their start and end apart: 3, of which 3 were waited for; matrix products, arithmetic and copies ran while one was open for 3% of the time, Pallas kernels for 0%

profile of v1, /device:TPU:4, one launch (start us, length us, event | category | flops | bytes accessed | tf_op | source)
XLA Modules:
  0.0 258.5 jit_solution(7130072115704097422)
XLA Ops:
  7.2 0.8 pad_maximum_fusion
  7.9 0.5 stack.2
  8.4 0.0 copy-start
  8.5 114.4 %all_to_all.10 = bf16[64,64,512]{2,1,0:T(8,128)(2,1)S(1)} all-to-all(bf16[64,64,512]{2,1,0:T(8,128)(2,1)S(1)} %stack.2), channel_id=1, replica_groups=mesh['vocab_0'=8,'vocab_1'=8,'pipe'=8] {'vocab_0','vocab_1'}, dimensions={0} | all-to-all | bytes 8388608 | tf_op jit(solution)/shard_map/all_to_all | solution.py:15
  122.8 0.0 copy-done
  122.8 1.3 fusion.61
  124.2 0.6 copy-done.1
  124.8 0.2 exponential_reduce_fusion
  125.0 0.7 broadcast_in_dim.7
  125.7 12.6 %all-to-all-start.1 = ((f32[64,2,256]{2,1,0:T(2,128)}), f32[64,2,256]{2,1,0:T(2,128)S(1)}, u32[]{:S(2)}, u32[]{:S(2)}) async-start(f32[64,2,256]{2,1,0:T(2,128)} %broadcast_in_dim.7), calls=%async_computation.1 | async-start | bytes 262144 | tf_op jit(solution)/shard_map/all_to_all | solution.py:55
  138.3 0.0 reduce-scatter.5.cloned.1.call-start
  138.4 12.7 %all-to-all-done.1 = f32[64,2,256]{2,1,0:T(2,128)S(1)} async-done(((f32[64,2,256]{2,1,0:T(2,128)}), f32[64,2,256]{2,1,0:T(2,128)S(1)}, u32[]{:S(2)}, u32[]{:S(2)}) %all-to-all-start.1) | async-done | bytes 131104 | tf_op jit(solution)/shard_map/all_to_all | solution.py:55
  151.1 0.1 fusion.55
  151.7 5.5 %fusion.4 = f32[256,4096]{1,0:T(8,128)} fusion(bf16[4096,512]{1,0:T(8,128)(2,1)} %param.11, f32[256,512]{1,0:T(8,128)S(1)} %get-tuple-element.68, f32[256]{0:T(256)S(1)} %copy-done.2, f32[256]{0:T(256)S(1)} %bitcast.215, f32[256]{0:T(256)S(1)} %bitcast.216, s32[512]{0:T(512)S(1)} %iota_add_fusion, s32[256]{0:T(256)S(1)} %copy-done.3), kind=kOutput, calls=%fused_computation.9 | convolution fusion | flops 1074659328 | bytes 8919040 | tf_op jit(solution)/shard_map/dot_general | solution.py:129
  157.2 0.0 reduce-scatter.5.cloned.1.call-update
  157.3 0.0 copy-start.4
  157.3 0.0 reduce-scatter.7.cloned.1.call-start
  157.3 4.2 %fusion.60 = (f32[256]{0:T(256)S(1)}, f32[256,512]{1,0:T(8,128)S(1)}) fusion(bf16[4096,512]{1,0:T(8,128)(2,1)} %param.11, bf16[4096,512]{1,0:T(8,128)(2,1)} %bitcast.210), kind=kOutput, calls=%fused_computation.119 | convolution fusion | flops 1073872640 | bytes 6816768 | tf_op jit(solution)/shard_map/dot_general | solution.py:110
  161.5 0.0 copy-done.4
  161.5 1.5 exponential_reduce_fusion.1
  163.0 0.6 pad.7
  163.7 25.2 %all-gather.2 = f32[8,4,256]{2,1,0:T(4,128)S(1)} all-gather(f32[1,4,256]{2,1,0:T(4,128)S(1)} %maximum_bitcast_fusion), channel_id=2, replica_groups=mesh['vocab_0'=8,'vocab_1'=8,'pipe'=8] {'vocab_0'}, dimensions={0}, use_global_device_ids=true | all-gather | bytes 36864 | tf_op jit(solution)/shard_map/all_gather | solution.py:35
  189.0 0.6 fusion.59
  194.6 13.4 %reduce-scatter.5.cloned.1.call-done = f32[256,512]{1,0:T(8,128)} async-done(((f32[256,4096]{1,0:T(8,128)}), f32[256,512]{1,0:T(8,128)}) %reduce-scatter.5.cloned.1.call-update) | async-done | bytes 524304 | tf_op jit(solution)/shard_map/reduce_scatter | solution.py:90
  207.9 2.0 copy.14
  210.0 0.0 reduce-scatter.7.cloned.1.call-update
  210.0 25.7 %all-gather.3 = f32[8,4,256]{2,1,0:T(4,128)S(1)} all-gather(f32[1,4,256]{2,1,0:T(4,128)S(1)} %maximum_bitcast_fusion.1), channel_id=3, replica_groups=mesh['vocab_0'=8,'vocab_1'=8,'pipe'=8] {'vocab_1'}, dimensions={0}, use_global_device_ids=true | all-gather | bytes 36864 | tf_op jit(solution)/shard_map/all_gather | solution.py:35
  235.7 0.6 fusion.58
  241.5 0.6 add_subtract_fusion
  242.1 6.8 %reduce-scatter.7.cloned.1.call-done = f32[64,256]{1,0:T(8,128)} async-done(((f32[512,256]{1,0:T(8,128)}), f32[64,256]{1,0:T(8,128)}) %reduce-scatter.7.cloned.1.call-update) | async-done | bytes 65552
  248.9 0.9 copy.15
  249.8 0.7 copy.13
  (45 shorter events, 0.6 us)
Async XLA Ops:
  8.4 114.4 %copy-start = (bf16[4096,512]{1,0:T(8,128)(2,1)S(1)}, bf16[4096,512]{1,0:T(8,128)(2,1)}, u32[]{:S(2)}) copy-start(bf16[4096,512]{1,0:T(8,128)(2,1)} %param.11) | copy-start | bytes 12582916
  122.8 2.0 copy-start.1
  122.8 28.9 %copy-start.2 = (f32[256]{0:T(256)S(1)}, f32[256]{0:T(256)}, u32[]{:S(2)}) copy-start(f32[256]{0:T(256)} %param.10) | copy-start | bytes 3076
  122.8 28.9 %copy-start.3 = (s32[256]{0:T(256)S(1)}, s32[256]{0:T(256)}, u32[]{:S(2)}) copy-start(s32[256]{0:T(256)} %param.9) | copy-start | bytes 3076
  125.7 25.3 %all-to-all-start.1 = ((f32[64,2,256]{2,1,0:T(2,128)}), f32[64,2,256]{2,1,0:T(2,128)S(1)}, u32[]{:S(2)}, u32[]{:S(2)}) async-start(f32[64,2,256]{2,1,0:T(2,128)} %broadcast_in_dim.7), calls=%async_computation.1 | async-start | bytes 262144 | tf_op jit(solution)/shard_map/all_to_all | solution.py:55
  138.3 69.6 %reduce-scatter.5.cloned.1.call-start = ((), (), s32[]{:S(2)}) async-start(), calls=%async_computation.4 | async-start | bytes 4718592 | tf_op jit(solution)/shard_map/reduce_scatter | solution.py:90
  157.3 4.2 %copy-start.4 = (s32[256]{0:T(256)S(1)}, s32[256]{0:T(256)}, u32[]{:S(2)}) copy-start(s32[256]{0:T(256)} %param.7) | copy-start | bytes 3076
  157.3 91.6 %reduce-scatter.7.cloned.1.call-start = ((), (), s32[]{:S(2)}) async-start(), calls=%async_computation.5 | async-start | bytes 589824
Sparse Core Ops, SparseCore 0:
  157.4 50.5 reduce-scatter.4
  210.7 38.0 reduce-scatter.6
